TPU v7x, 512 devices: a whole 4x8x8 slice. The times are simulated.
512 devices in a mesh: gx: 8 (over z), gy: 4 (over y_hi), gz: 16 (over y_lo, x, core).
Axes of the slice: x: 4, y: 8 (y_hi: 4, y_lo: 2; y = y_hi * 2 + y_lo), z: 8, core: 2. Of those that a mesh axis runs over, the one named last changes fastest.
Arguments:
- schur: bfloat16 [8, 4, 16, 1024, 1024], P('gx', 'gy', 'gz'), may hold values from -0.2 to 2.7
- block_map: int32 [8, 4, 16, 26], P('gx', 'gy', 'gz'), may hold values from 0 to 7
- vectors: bfloat16 [8, 4, 16, 1024, 512], P('gx', 'gy', 'gz'), may hold values from -3 to 3
Outputs:
- assembled: bfloat16 [8, 4, 16, 1024, 512], P('gx', 'gy', 'gz')
- update: bfloat16 [8, 4, 16, 1024, 512], P('gx', 'gy', 'gz')
All inputs are finite; a program needn't handle non-finite values.
Results may differ from a plain program's by a relative error of at most 0.0056.
Values may be sent and summed in bfloat16 or wider, within the bound.
No kernel may reach another device: no remote copies, remote signals or barrier semaphores. Data moves between devices by JAX's collectives and lax.ppermute only.
A program may use at most 64 MiB of HBM per device.

v0:
```python
import functools

import jax
import jax.numpy as jnp
from jax import lax
from jax.experimental import pallas as pl
from jax.experimental.pallas import tpu as pltpu
from jax.sharding import PartitionSpec as P


BLOCK = 128
HALF = BLOCK // 2
STEPS = (-1, 0, 1)
LINKS = 26
NOTE = 16
MIB = 1024 * 1024
AXES = ("gx", "gy", "gz")


def link(a, b, c):
    place = 9 * (a + 1) + 3 * (b + 1) + (c + 1)
    if isinstance(place, int):
        return place if place < 13 else place - 1
    return jnp.where(place < 13, place, place - 1)


def cell(first, second):
    return 3 * (first + 1) + (second + 1)


def side(here, axis):
    return 1 - 2 * (here[axis][0] % 2)


def part(stack, index):
    start = index * HALF
    if not isinstance(start, int):
        start = pl.multiple_of(start, HALF)
    return stack[pl.ds(start, HALF), :]


def swap(near, far, axis, ring):
    count = lax.axis_size(axis)
    got = []
    for value, first in ((near, 0), (far, 1)):
        pairs = []
        for low in range(first, count, 2):
            high = (low + 1) % count
            if low + 1 < count or ring:
                pairs += [(low, high), (high, low)]
        got.append(lax.ppermute(value, axis, pairs))
    return got


def head_kernel(links, x, y, z, schur, vectors, top, bottom, near_a, far_a, matrix, right_side, sems):
    blocks = bottom.shape[0]
    copies = [pltpu.make_async_copy(vectors, right_side, sems.at[blocks])]
    for k in range(blocks):
        rows = slice(k * BLOCK, (k + 1) * BLOCK)
        copies.append(pltpu.make_async_copy(schur.at[rows, :], matrix.at[rows, :], sems.at[k]))
    for copy in copies:
        copy.start()
    lane = lax.broadcasted_iota(jnp.int32, (NOTE, top.shape[1]), 1)
    note = jnp.zeros((NOTE, top.shape[1]), jnp.int32)
    for i in range(LINKS):
        note = jnp.where(lane == i, links[i], note)
    top[blocks * HALF :, :] = note.astype(jnp.float32).astype(jnp.bfloat16)
    copies[0].wait()
    for k in range(blocks):
        rows = slice(k * BLOCK, (k + 1) * BLOCK)
        copies[k + 1].wait()
        product = jnp.dot(
            matrix[rows, :], right_side[...], preferred_element_type=jnp.float32
        ).astype(jnp.bfloat16)
        diagonal = matrix[rows, rows]
        upper = slice(k * HALF, (k + 1) * HALF)
        top[upper, BLOCK:] = product[:HALF]
        top[upper, :BLOCK] = diagonal[:HALF]
        bottom[k, :, BLOCK:] = product[HALF:]
        bottom[k, :, :BLOCK] = diagonal[HALF:]
    sx = side((x, y, z), 0)
    for a, out in ((sx, near_a), (-sx, far_a)):
        for b in STEPS:
            for c in STEPS:
                out[cell(b, c)] = bottom[links[link(a, b, c)]]


def first_a_kernel(
    links, x, y, z, top, near_b, far_b, near_a, far_a, near_links, far_links, notes, sems
):
    rows = top.shape[0] - NOTE
    copies = []
    for i, (source, out) in enumerate(((near_b, near_links), (far_b, far_links))):
        notes[i] = source[rows : rows + 8, :BLOCK].astype(jnp.float32).astype(jnp.int32)
        copies.append(pltpu.make_async_copy(notes.at[i], out, sems.at[i]))
        copies[-1].start()
    sx, sy = side((x, y, z), 0), side((x, y, z), 1)
    for a, out in ((sx, near_a), (-sx, far_a)):
        for c in STEPS:
            out[cell(0, c)] = part(top, links[link(a, 0, c)])
    for copy in copies:
        copy.wait()
    for a, out in ((sx, near_a), (-sx, far_a)):
        for b, source, there in ((-sy, near_b, near_links), (sy, far_b, far_links)):
            for c in STEPS:
                out[cell(b, c)] = part(source, there[0, link(a, b, c)])


def ahead_c_kernel(
    links, x, y, z, near_links, far_links, top, bottom, near_b, far_b, near_a, far_a, near_c, far_c
):
    sx, sy, sz = side((x, y, z), 0), side((x, y, z), 1), side((x, y, z), 2)
    for c, out in ((-sz, far_c), (sz, near_c)):
        out[1] = part(top, links[link(0, 0, c)])
        out[4] = bottom[links[link(0, 0, c)]]
        for b, source, there in ((-sy, near_b, near_links), (sy, far_b, far_links)):
            out[b + 1] = part(source, there[0, link(0, b, c)])
        for a, source in ((-sx, near_a), (sx, far_a)):
            out[a + 4] = source[cell(0, c)]


def late_c_kernel(axis, x, y, z, near, far, near_c, far_c):
    step, sz = side((x, y, z), axis), side((x, y, z), 2)
    for c, out in ((-sz, far_c), (sz, near_c)):
        for motion, source in ((-step, near), (step, far)):
            for other in STEPS:
                out[3 * ((motion + 1) // 2) + other + 1] = source[cell(other, c)]


def second_b_kernel(links, x, y, z, bottom, near_a, far_a, near_b, far_b):
    sx, sy = side((x, y, z), 0), side((x, y, z), 1)
    for b, out in ((sy, near_b), (-sy, far_b)):
        for c in STEPS:
            out[cell(0, c)] = bottom[links[link(0, b, c)]]
            for a, source in ((-sx, near_a), (sx, far_a)):
                out[cell(a, c)] = source[cell(b, c)]


def add_into(sums, slot, piece):
    sums[slot] = sums[slot] + piece.astype(jnp.float32)


def seed_kernel(links, x, y, z, bottom, near_a, far_a, lower):
    sx = side((x, y, z), 0)
    lower[...] = bottom[...].astype(jnp.float32)
    for a, source in ((-sx, near_a), (sx, far_a)):
        add_into(lower, links[link(-a, 0, 0)], source[cell(0, 0)])


def lower_kernel(links, x, y, z, seed, near_b, far_b, near_ahead, far_ahead, lower):
    sy, sz = side((x, y, z), 1), side((x, y, z), 2)
    lower[...] = seed[...]
    for b, source in ((-sy, near_b), (sy, far_b)):
        for a in STEPS:
            add_into(lower, links[link(-a, -b, 0)], source[cell(a, 0)])
    for c, source in ((-sz, near_ahead), (sz, far_ahead)):
        for a in STEPS:
            add_into(lower, links[link(-a, 0, -c)], source[a + 4])


def upper_kernel(
    links,
    x,
    y,
    z,
    near_links,
    far_links,
    top,
    near_b,
    far_b,
    near_a,
    far_a,
    near_ahead,
    far_ahead,
    near_c,
    far_c,
    upper,
):
    sx, sy, sz = side((x, y, z), 0), side((x, y, z), 1), side((x, y, z), 2)
    for k in range(upper.shape[0]):
        upper[k] = part(top, k).astype(jnp.float32)
    for b, source, there in ((-sy, near_b, near_links), (sy, far_b, far_links)):
        add_into(upper, links[link(0, -b, 0)], part(source, there[0, link(0, b, 0)]))
    for a, source in ((-sx, near_a), (sx, far_a)):
        for b in STEPS:
            add_into(upper, links[link(-a, -b, 0)], source[cell(b, 0)])
    for c, ahead, source in ((-sz, near_ahead, near_c), (sz, far_ahead, far_c)):
        for b in STEPS:
            add_into(upper, links[link(0, -b, -c)], ahead[b + 1])
            add_into(upper, links[link(1, -b, -c)], source[b + 1])
            add_into(upper, links[link(-1, -b, -c)], source[b + 4])


def tail_kernel(
    columns,
    layers,
    links,
    x,
    y,
    z,
    upper,
    lower,
    near_c,
    far_c,
    schur,
    assembled,
    update,
    under,
    summed_rows,
    scaled,
    update_rows,
    counts,
    sems,
):
    blocks = upper.shape[0]
    row, layer = y[0], z[0]
    sz = side((x, y, z), 2)
    for k in range(blocks):
        counts[k] = 1
    for a in STEPS:
        for b in STEPS:
            for c in STEPS:
                if (a, b, c) == (0, 0, 0):
                    continue
                slot = links[link(a, b, c)]
                alive = (row + b >= 0) & (row + b < columns) & (layer + c >= 0) & (layer + c < layers)
                counts[slot] = counts[slot] + jnp.where(alive, 1, 0)
    under[...] = lower[...]
    for c, source in ((-sz, near_c), (sz, far_c)):
        for a in STEPS:
            add_into(under, links[link(-a, 1, -c)], source[a + 1])
            add_into(under, links[link(-a, -1, -c)], source[a + 4])
    copies = []
    for k in range(blocks):
        rows = slice(k * BLOCK, (k + 1) * BLOCK)
        whole = jnp.concatenate([upper[k], under[k]], axis=0)
        coupling = whole[:, :BLOCK]
        summed = whole[:, BLOCK:]
        summed_high = summed.astype(jnp.bfloat16)
        summed_low = (summed - summed_high.astype(jnp.float32)).astype(jnp.bfloat16)
        coupling_high = coupling.astype(jnp.bfloat16)
        coupling_low = (coupling - coupling_high.astype(jnp.float32)).astype(jnp.bfloat16)
        summed_rows[rows, :] = summed_high
        copies.append(
            pltpu.make_async_copy(summed_rows.at[rows, :], assembled.at[rows, :], sems.at[k])
        )
        copies[-1].start()
        mixed = jnp.dot(coupling_high, summed_high, preferred_element_type=jnp.float32)
        mixed += jnp.dot(coupling_high, summed_low, preferred_element_type=jnp.float32)
        mixed += jnp.dot(coupling_low, summed_high, preferred_element_type=jnp.float32)
        share = jnp.full((BLOCK, 1), counts[k], jnp.int32).astype(jnp.float32)
        scaled[rows, :] = (mixed / share).astype(jnp.bfloat16)
    for k in range(blocks):
        rows = slice(k * BLOCK, (k + 1) * BLOCK)
        update_rows[rows, :] = jnp.dot(
            schur[rows, :], scaled[...], preferred_element_type=jnp.float32
        ).astype(jnp.bfloat16)
        copies.append(
            pltpu.make_async_copy(update_rows.at[rows, :], update.at[rows, :], sems.at[blocks + k])
        )
        copies[-1].start()
    for copy in copies:
        copy.wait()


def call(kernel, outs, *operands, smem=4, scratch=(), room=4, far_in=0, far_out=False, notes=0):
    near = pl.BlockSpec(memory_space=pltpu.VMEM)
    far = pl.BlockSpec(memory_space=pltpu.HBM)
    specs = [pl.BlockSpec(memory_space=pltpu.SMEM)] * smem
    specs += [near] * (len(operands) - smem - far_in) + [far] * far_in
    return pl.pallas_call(
        kernel,
        out_shape=outs,
        in_specs=specs,
        out_specs=[far if far_out else near] * (len(outs) - notes)
        + [pl.BlockSpec(memory_space=pltpu.SMEM)] * notes,
        scratch_shapes=list(scratch),
        compiler_params=pltpu.CompilerParams(vmem_limit_bytes=room * MIB),
    )(*operands)


def local(schur, block_map, vectors):
    matrix = schur[0, 0, 0]
    right_side = vectors[0, 0, 0]
    order, width = right_side.shape
    blocks = order // BLOCK
    full = BLOCK + width
    nine = [jax.ShapeDtypeStruct((9, HALF, full), jnp.bfloat16)] * 2
    six = [jax.ShapeDtypeStruct((6, HALF, full), jnp.bfloat16)] * 2
    half = [jax.ShapeDtypeStruct((blocks, HALF, full), jnp.float32)]
    place = [lax.axis_index(axis).astype(jnp.int32).reshape(1) for axis in AXES]
    here = [block_map[0, 0, 0]] + place

    top, bottom, *sent = call(
        head_kernel,
        [
            jax.ShapeDtypeStruct((blocks * HALF + NOTE, full), jnp.bfloat16),
            jax.ShapeDtypeStruct((blocks, HALF, full), jnp.bfloat16),
        ]
        + nine,
        *here,
        matrix,
        right_side,
        far_in=2,
        scratch=[
            pltpu.VMEM((order, order), jnp.bfloat16),
            pltpu.VMEM((order, width), jnp.bfloat16),
            pltpu.SemaphoreType.DMA((blocks + 1,)),
        ],
        room=51,
    )
    first_b = swap(top, top, "gy", False)
    second_a = swap(*sent, "gx", True)
    sent = call(second_b_kernel, nine, *here, bottom, *second_a)
    second_b = swap(*sent, "gy", False)
    (seed,) = call(seed_kernel, half, *here, bottom, *second_a)
    *sent, near_links, far_links = call(
        first_a_kernel,
        nine + [jax.ShapeDtypeStruct((8, BLOCK), jnp.int32)] * 2,
        *here,
        top,
        *first_b,
        scratch=[pltpu.VMEM((2, 8, BLOCK), jnp.int32), pltpu.SemaphoreType.DMA((2,))],
        notes=2,
    )
    first_a = swap(*sent, "gx", True)
    maps = [*here, near_links, far_links]
    sent = call(ahead_c_kernel, six, *maps, top, bottom, *first_b, *second_a, smem=6)
    ahead_c = swap(*sent, "gz", False)
    sent = call(functools.partial(late_c_kernel, 0), six, *place, *first_a, smem=3)
    first_c = swap(*sent, "gz", False)
    sent = call(functools.partial(late_c_kernel, 1), six, *place, *second_b, smem=3)
    second_c = swap(*sent, "gz", False)
    (lower,) = call(lower_kernel, half, *here, seed, *second_b, *ahead_c)
    (upper,) = call(upper_kernel, half, *maps, top, *first_b, *first_a, *ahead_c, *first_c, smem=6)
    assembled, update = call(
        functools.partial(tail_kernel, lax.axis_size("gy"), lax.axis_size("gz")),
        [jax.ShapeDtypeStruct((order, width), jnp.bfloat16)] * 2,
        *here,
        upper,
        lower,
        *second_c,
        matrix,
        scratch=[
            pltpu.VMEM((blocks, HALF, full), jnp.float32),
            pltpu.VMEM((order, width), jnp.bfloat16),
            pltpu.VMEM((order, width), jnp.bfloat16),
            pltpu.VMEM((order, width), jnp.bfloat16),
            pltpu.SMEM((blocks,), jnp.int32),
            pltpu.SemaphoreType.DMA((2 * blocks,)),
        ],
        room=12,
        far_out=True,
    )
    return (assembled[None, None, None], update[None, None, None])


def solution(mesh):
    placed = (
        P("gx", "gy", "gz", None, None),
        P("gx", "gy", "gz", None),
        P("gx", "gy", "gz", None, None),
    )

    return jax.shard_map(
        local,
        mesh=mesh,
        in_specs=placed,
        out_specs=(P("gx", "gy", "gz", None, None), P("gx", "gy", "gz", None, None)),
        check_vma=False,
    )
```

profile of v0, /device:TPU:24, one launch (start us, length us, event | category | flops | bytes accessed | tf_op | source)
XLA Modules:
  0.0 122.4 jit_solution(18253016842695543952)
XLA Ops:
  0.6 0.0 copy-start.1
  0.6 0.6 copy-done.1
  1.3 4.5 %shard_map.50 = (bf16[528,640]{1,0:T(8,128)(2,1)S(1)}, bf16[8,64,640]{2,1,0:T(8,128)(2,1)S(1)}, bf16[9,64,640]{2,1,0:T(8,128)(2,1)S(1)}, bf16[9,64,640]{2,1,0:T(8,128)(2,1)S(1)}) custom-call(s32[26]{0:T(128)S(1)} %bitcast.10, s32[1]{0:T(128)} %bitcast.1.x, s32[1]{0:T(128)} %bitcast.2.y, s32[1]{0:T(128)} %bitcast.3.z, bf16[1024,1024]{1,0:T(8,128)(2,1)} %bitcast.8, ...), custom_call_target="tpu_custom_call" | custom-call | tf_op jit(solution)/shard_map/pallas_call | solution.py:271
  5.8 4.3 %collective-permute-start.4 = (bf16[9,64,640]{2,1,0:T(8,128)(2,1)S(1)}, bf16[9,64,640]{2,1,0:T(8,128)(2,1)S(1)}, u32[]{:S(2)}, u32[]{:S(2)}) collective-permute-start(bf16[9,64,640]{2,1,0:T(8,128)(2,1)S(1)} %get-tuple-element.26), channel_id=1, source_target_pairs={{0,64},{64,0},{128,192},{192,128},{256,320},{320,256},{384,448},{4... | collective-permute-start | bytes 2211848 | tf_op jit(solution)/shard_map/ppermute | solution.py:51
  10.1 9.1 %collective-permute-start.5 = (bf16[9,64,640]{2,1,0:T(8,128)(2,1)S(1)}, bf16[9,64,640]{2,1,0:T(8,128)(2,1)S(1)}, u32[]{:S(2)}, u32[]{:S(2)}) collective-permute-start(bf16[9,64,640]{2,1,0:T(8,128)(2,1)S(1)} %get-tuple-element.27), channel_id=1, source_target_pairs={{64,128},{128,64},{192,256},{256,192},{320,384},{384,320},{448,0},... | collective-permute-start | bytes 2211848 | tf_op jit(solution)/shard_map/ppermute | solution.py:51
  19.3 2.2 %collective-permute-start = (bf16[528,640]{1,0:T(8,128)(2,1)S(1)}, bf16[528,640]{1,0:T(8,128)(2,1)S(1)}, u32[]{:S(2)}, u32[]{:S(2)}) collective-permute-start(bf16[528,640]{1,0:T(8,128)(2,1)S(1)} %get-tuple-element.20.top), channel_id=1, source_target_pairs={{0,16},{16,0},{32,48},{48,32},{1,17},{17,1},{33,49},{49,33},{2,18}... | collective-permute-start | bytes 2027528 | tf_op jit(solution)/shard_map/ppermute | solution.py:51
  21.5 5.3 %collective-permute-start.1 = (bf16[528,640]{1,0:T(8,128)(2,1)S(1)}, bf16[528,640]{1,0:T(8,128)(2,1)S(1)}, u32[]{:S(2)}, u32[]{:S(2)}) collective-permute-start(bf16[528,640]{1,0:T(8,128)(2,1)S(1)} %get-tuple-element.20.top), channel_id=1, source_target_pairs={{16,32},{32,16},{17,33},{33,17},{18,34},{34,18},{19,35},{35,19},{2... | collective-permute-start | bytes 2027528 | tf_op jit(solution)/shard_map/ppermute | solution.py:51
  26.8 26.1 %collective-permute-done.near_b = bf16[528,640]{1,0:T(8,128)(2,1)S(1)} collective-permute-done((bf16[528,640]{1,0:T(8,128)(2,1)S(1)}, bf16[528,640]{1,0:T(8,128)(2,1)S(1)}, u32[]{:S(2)}, u32[]{:S(2)}) %collective-permute-start) | collective-permute-done | bytes 675872 | tf_op jit(solution)/shard_map/ppermute | solution.py:51
  52.9 3.0 %collective-permute-done.1.far_b = bf16[528,640]{1,0:T(8,128)(2,1)S(1)} collective-permute-done((bf16[528,640]{1,0:T(8,128)(2,1)S(1)}, bf16[528,640]{1,0:T(8,128)(2,1)S(1)}, u32[]{:S(2)}, u32[]{:S(2)}) %collective-permute-start.1) | collective-permute-done | bytes 675872 | tf_op jit(solution)/shard_map/ppermute | solution.py:51
  55.9 2.0 %shard_map.51 = (bf16[9,64,640]{2,1,0:T(8,128)(2,1)S(1)}, bf16[9,64,640]{2,1,0:T(8,128)(2,1)S(1)}, s32[8,128]{1,0:T(8,128)S(1)}, s32[8,128]{1,0:T(8,128)S(1)}) custom-call(s32[26]{0:T(128)S(1)} %bitcast.11, s32[1]{0:T(128)} %bitcast.1.x, s32[1]{0:T(128)} %bitcast.2.y, s32[1]{0:T(128)} %bitcast.3.z, bf16[528,640]{1,0:T(8,128)(2,1)S(1)} %get-tuple-element.20.top, ...), custom_call_target="tpu_custom_call" | custom-call | tf_op jit(solution)/shard_map/pallas_call | solution.py:271
  57.9 1.9 %collective-permute-start.2 = (bf16[9,64,640]{2,1,0:T(8,128)(2,1)S(1)}, bf16[9,64,640]{2,1,0:T(8,128)(2,1)S(1)}, u32[]{:S(2)}, u32[]{:S(2)}) collective-permute-start(bf16[9,64,640]{2,1,0:T(8,128)(2,1)S(1)} %get-tuple-element.23), channel_id=1, source_target_pairs={{0,64},{64,0},{128,192},{192,128},{256,320},{320,256},{384,448},{4... | collective-permute-start | bytes 2211848 | tf_op jit(solution)/shard_map/ppermute | solution.py:51
  59.8 3.7 %collective-permute-start.3 = (bf16[9,64,640]{2,1,0:T(8,128)(2,1)S(1)}, bf16[9,64,640]{2,1,0:T(8,128)(2,1)S(1)}, u32[]{:S(2)}, u32[]{:S(2)}) collective-permute-start(bf16[9,64,640]{2,1,0:T(8,128)(2,1)S(1)} %get-tuple-element.24), channel_id=1, source_target_pairs={{64,128},{128,64},{192,256},{256,192},{320,384},{384,320},{448,0},... | collective-permute-start | bytes 2211848 | tf_op jit(solution)/shard_map/ppermute | solution.py:51
  63.5 0.0 collective-permute-done.4.near_a
  63.5 0.0 collective-permute-done.5.far_a
  63.5 0.7 shard_map.56
  64.2 1.9 %collective-permute-start.10 = (bf16[9,64,640]{2,1,0:T(8,128)(2,1)S(1)}, bf16[9,64,640]{2,1,0:T(8,128)(2,1)S(1)}, u32[]{:S(2)}, u32[]{:S(2)}) collective-permute-start(bf16[9,64,640]{2,1,0:T(8,128)(2,1)S(1)} %get-tuple-element.32), channel_id=1, source_target_pairs={{0,16},{16,0},{32,48},{48,32},{1,17},{17,1},{33,49},{49,33},{2,18}... | collective-permute-start | bytes 2211848 | tf_op jit(solution)/shard_map/ppermute | solution.py:51
  66.1 2.6 %collective-permute-start.11 = (bf16[9,64,640]{2,1,0:T(8,128)(2,1)S(1)}, bf16[9,64,640]{2,1,0:T(8,128)(2,1)S(1)}, u32[]{:S(2)}, u32[]{:S(2)}) collective-permute-start(bf16[9,64,640]{2,1,0:T(8,128)(2,1)S(1)} %get-tuple-element.33), channel_id=1, source_target_pairs={{16,32},{32,16},{17,33},{33,17},{18,34},{34,18},{19,35},{35,19},{2... | collective-permute-start | bytes 2211848 | tf_op jit(solution)/shard_map/ppermute | solution.py:51
  68.7 0.8 shard_map.52
  69.5 1.9 %collective-permute-start.6 = (bf16[6,64,640]{2,1,0:T(8,128)(2,1)S(1)}, bf16[6,64,640]{2,1,0:T(8,128)(2,1)S(1)}, u32[]{:S(2)}, u32[]{:S(2)}) collective-permute-start(bf16[6,64,640]{2,1,0:T(8,128)(2,1)S(1)} %get-tuple-element.28), channel_id=1, source_target_pairs={{0,1},{1,0},{2,3},{3,2},{4,5},{5,4},{6,7},{7,6},{8,9},{9,8},{10,11... | collective-permute-start | bytes 1474568 | tf_op jit(solution)/shard_map/ppermute | solution.py:51
  71.4 3.7 %collective-permute-done.2.near.near_a = bf16[9,64,640]{2,1,0:T(8,128)(2,1)S(1)} collective-permute-done((bf16[9,64,640]{2,1,0:T(8,128)(2,1)S(1)}, bf16[9,64,640]{2,1,0:T(8,128)(2,1)S(1)}, u32[]{:S(2)}, u32[]{:S(2)}) %collective-permute-start.2) | collective-permute-done | bytes 737312 | tf_op jit(solution)/shard_map/ppermute | solution.py:51
  75.1 5.0 %collective-permute-start.7 = (bf16[6,64,640]{2,1,0:T(8,128)(2,1)S(1)}, bf16[6,64,640]{2,1,0:T(8,128)(2,1)S(1)}, u32[]{:S(2)}, u32[]{:S(2)}) collective-permute-start(bf16[6,64,640]{2,1,0:T(8,128)(2,1)S(1)} %get-tuple-element.29), channel_id=1, source_target_pairs={{1,2},{2,1},{3,4},{4,3},{5,6},{6,5},{7,8},{8,7},{9,10},{10,9},{11,... | collective-permute-start | bytes 1474568 | tf_op jit(solution)/shard_map/ppermute | solution.py:51
  80.2 0.0 collective-permute-done.3.far.far_a
  80.2 0.1 shard_map.53
  80.3 1.9 %collective-permute-start.8 = (bf16[6,64,640]{2,1,0:T(8,128)(2,1)S(1)}, bf16[6,64,640]{2,1,0:T(8,128)(2,1)S(1)}, u32[]{:S(2)}, u32[]{:S(2)}) collective-permute-start(bf16[6,64,640]{2,1,0:T(8,128)(2,1)S(1)} %get-tuple-element.30), channel_id=1, source_target_pairs={{0,1},{1,0},{2,3},{3,2},{4,5},{5,4},{6,7},{7,6},{8,9},{9,8},{10,11... | collective-permute-start | bytes 1474568 | tf_op jit(solution)/shard_map/ppermute | solution.py:51
  82.2 15.4 %collective-permute-done.10.near_b.near = bf16[9,64,640]{2,1,0:T(8,128)(2,1)S(1)} collective-permute-done((bf16[9,64,640]{2,1,0:T(8,128)(2,1)S(1)}, bf16[9,64,640]{2,1,0:T(8,128)(2,1)S(1)}, u32[]{:S(2)}, u32[]{:S(2)}) %collective-permute-start.10) | collective-permute-done | bytes 737312 | tf_op jit(solution)/shard_map/ppermute | solution.py:51
  97.6 2.0 %collective-permute-start.9 = (bf16[6,64,640]{2,1,0:T(8,128)(2,1)S(1)}, bf16[6,64,640]{2,1,0:T(8,128)(2,1)S(1)}, u32[]{:S(2)}, u32[]{:S(2)}) collective-permute-start(bf16[6,64,640]{2,1,0:T(8,128)(2,1)S(1)} %get-tuple-element.31), channel_id=1, source_target_pairs={{1,2},{2,1},{3,4},{4,3},{5,6},{6,5},{7,8},{8,7},{9,10},{10,9},{11,... | collective-permute-start | bytes 1474568 | tf_op jit(solution)/shard_map/ppermute | solution.py:51
  99.6 1.1 collective-permute-done.11.far_b.far
  100.7 0.1 shard_map.58
  100.8 2.4 %collective-permute-start.12 = (bf16[6,64,640]{2,1,0:T(8,128)(2,1)S(1)}, bf16[6,64,640]{2,1,0:T(8,128)(2,1)S(1)}, u32[]{:S(2)}, u32[]{:S(2)}) collective-permute-start(bf16[6,64,640]{2,1,0:T(8,128)(2,1)S(1)} %get-tuple-element.34), channel_id=1, source_target_pairs={{0,1},{1,0},{2,3},{3,2},{4,5},{5,4},{6,7},{7,6},{8,9},{9,8},{10,11... | collective-permute-start | bytes 1474568 | tf_op jit(solution)/shard_map/ppermute | solution.py:51
  103.2 0.0 collective-permute-done.6.near_ahead
  103.2 6.2 %collective-permute-start.13 = (bf16[6,64,640]{2,1,0:T(8,128)(2,1)S(1)}, bf16[6,64,640]{2,1,0:T(8,128)(2,1)S(1)}, u32[]{:S(2)}, u32[]{:S(2)}) collective-permute-start(bf16[6,64,640]{2,1,0:T(8,128)(2,1)S(1)} %get-tuple-element.35), channel_id=1, source_target_pairs={{1,2},{2,1},{3,4},{4,3},{5,6},{6,5},{7,8},{8,7},{9,10},{10,9},{11,... | collective-permute-start | bytes 1474568 | tf_op jit(solution)/shard_map/ppermute | solution.py:51
  109.4 0.7 shard_map.55.seed
  110.1 0.0 collective-permute-done.7.far_ahead
  110.1 0.8 shard_map.57.lower
  110.9 0.0 collective-permute-done.8.near_c
  110.9 2.4 %collective-permute-done.9.far_c = bf16[6,64,640]{2,1,0:T(8,128)(2,1)S(1)} collective-permute-done((bf16[6,64,640]{2,1,0:T(8,128)(2,1)S(1)}, bf16[6,64,640]{2,1,0:T(8,128)(2,1)S(1)}, u32[]{:S(2)}, u32[]{:S(2)}) %collective-permute-start.9) | collective-permute-done | bytes 491552 | tf_op jit(solution)/shard_map/ppermute | solution.py:51
  113.3 0.0 copy-start
  113.3 1.2 shard_map.54.upper
  114.5 0.0 collective-permute-done.12.near_c
  114.5 4.1 %collective-permute-done.13.far_c = bf16[6,64,640]{2,1,0:T(8,128)(2,1)S(1)} collective-permute-done((bf16[6,64,640]{2,1,0:T(8,128)(2,1)S(1)}, bf16[6,64,640]{2,1,0:T(8,128)(2,1)S(1)}, u32[]{:S(2)}, u32[]{:S(2)}) %collective-permute-start.13) | collective-permute-done | bytes 491552 | tf_op jit(solution)/shard_map/ppermute | solution.py:51
  118.6 0.0 copy-done
  118.6 3.8 %shard_map.59 = (bf16[1024,512]{1,0:T(8,128)(2,1)}, bf16[1024,512]{1,0:T(8,128)(2,1)}) custom-call(s32[26]{0:T(128)S(1)} %bitcast.17, s32[1]{0:T(128)} %bitcast.1.x, s32[1]{0:T(128)} %bitcast.2.y, s32[1]{0:T(128)} %bitcast.3.z, f32[8,64,640]{2,1,0:T(8,128)S(1)} %shard_map.54.upper, f32[8,64,640]{2,1,0:T(8,128)S(1)} %shard_map.57.lower, ...), custom_call_target="tpu_custom_call" | custom-call | tf_op jit(solution)/shard_map/pallas_call | solution.py:271
Async XLA Ops:
  0.6 0.7 copy-start.1
  5.8 57.6 %collective-permute-start.4 = (bf16[9,64,640]{2,1,0:T(8,128)(2,1)S(1)}, bf16[9,64,640]{2,1,0:T(8,128)(2,1)S(1)}, u32[]{:S(2)}, u32[]{:S(2)}) collective-permute-start(bf16[9,64,640]{2,1,0:T(8,128)(2,1)S(1)} %get-tuple-element.26), channel_id=1, source_target_pairs={{0,64},{64,0},{128,192},{192,128},{256,320},{320,256},{384,448},{4... | collective-permute-start | bytes 2211848 | tf_op jit(solution)/shard_map/ppermute | solution.py:51
  10.1 53.4 %collective-permute-start.5 = (bf16[9,64,640]{2,1,0:T(8,128)(2,1)S(1)}, bf16[9,64,640]{2,1,0:T(8,128)(2,1)S(1)}, u32[]{:S(2)}, u32[]{:S(2)}) collective-permute-start(bf16[9,64,640]{2,1,0:T(8,128)(2,1)S(1)} %get-tuple-element.27), channel_id=1, source_target_pairs={{64,128},{128,64},{192,256},{256,192},{320,384},{384,320},{448,0},... | collective-permute-start | bytes 2211848 | tf_op jit(solution)/shard_map/ppermute | solution.py:51
  19.3 33.6 %collective-permute-start = (bf16[528,640]{1,0:T(8,128)(2,1)S(1)}, bf16[528,640]{1,0:T(8,128)(2,1)S(1)}, u32[]{:S(2)}, u32[]{:S(2)}) collective-permute-start(bf16[528,640]{1,0:T(8,128)(2,1)S(1)} %get-tuple-element.20.top), channel_id=1, source_target_pairs={{0,16},{16,0},{32,48},{48,32},{1,17},{17,1},{33,49},{49,33},{2,18}... | collective-permute-start | bytes 2027528 | tf_op jit(solution)/shard_map/ppermute | solution.py:51
  21.5 34.4 %collective-permute-start.1 = (bf16[528,640]{1,0:T(8,128)(2,1)S(1)}, bf16[528,640]{1,0:T(8,128)(2,1)S(1)}, u32[]{:S(2)}, u32[]{:S(2)}) collective-permute-start(bf16[528,640]{1,0:T(8,128)(2,1)S(1)} %get-tuple-element.20.top), channel_id=1, source_target_pairs={{16,32},{32,16},{17,33},{33,17},{18,34},{34,18},{19,35},{35,19},{2... | collective-permute-start | bytes 2027528 | tf_op jit(solution)/shard_map/ppermute | solution.py:51
  57.9 17.2 %collective-permute-start.2 = (bf16[9,64,640]{2,1,0:T(8,128)(2,1)S(1)}, bf16[9,64,640]{2,1,0:T(8,128)(2,1)S(1)}, u32[]{:S(2)}, u32[]{:S(2)}) collective-permute-start(bf16[9,64,640]{2,1,0:T(8,128)(2,1)S(1)} %get-tuple-element.23), channel_id=1, source_target_pairs={{0,64},{64,0},{128,192},{192,128},{256,320},{320,256},{384,448},{4... | collective-permute-start | bytes 2211848 | tf_op jit(solution)/shard_map/ppermute | solution.py:51
  59.8 20.4 %collective-permute-start.3 = (bf16[9,64,640]{2,1,0:T(8,128)(2,1)S(1)}, bf16[9,64,640]{2,1,0:T(8,128)(2,1)S(1)}, u32[]{:S(2)}, u32[]{:S(2)}) collective-permute-start(bf16[9,64,640]{2,1,0:T(8,128)(2,1)S(1)} %get-tuple-element.24), channel_id=1, source_target_pairs={{64,128},{128,64},{192,256},{256,192},{320,384},{384,320},{448,0},... | collective-permute-start | bytes 2211848 | tf_op jit(solution)/shard_map/ppermute | solution.py:51
  64.2 33.5 %collective-permute-start.10 = (bf16[9,64,640]{2,1,0:T(8,128)(2,1)S(1)}, bf16[9,64,640]{2,1,0:T(8,128)(2,1)S(1)}, u32[]{:S(2)}, u32[]{:S(2)}) collective-permute-start(bf16[9,64,640]{2,1,0:T(8,128)(2,1)S(1)} %get-tuple-element.32), channel_id=1, source_target_pairs={{0,16},{16,0},{32,48},{48,32},{1,17},{17,1},{33,49},{49,33},{2,18}... | collective-permute-start | bytes 2211848 | tf_op jit(solution)/shard_map/ppermute | solution.py:51
  66.1 34.6 %collective-permute-start.11 = (bf16[9,64,640]{2,1,0:T(8,128)(2,1)S(1)}, bf16[9,64,640]{2,1,0:T(8,128)(2,1)S(1)}, u32[]{:S(2)}, u32[]{:S(2)}) collective-permute-start(bf16[9,64,640]{2,1,0:T(8,128)(2,1)S(1)} %get-tuple-element.33), channel_id=1, source_target_pairs={{16,32},{32,16},{17,33},{33,17},{18,34},{34,18},{19,35},{35,19},{2... | collective-permute-start | bytes 2211848 | tf_op jit(solution)/shard_map/ppermute | solution.py:51
  69.5 33.7 %collective-permute-start.6 = (bf16[6,64,640]{2,1,0:T(8,128)(2,1)S(1)}, bf16[6,64,640]{2,1,0:T(8,128)(2,1)S(1)}, u32[]{:S(2)}, u32[]{:S(2)}) collective-permute-start(bf16[6,64,640]{2,1,0:T(8,128)(2,1)S(1)} %get-tuple-element.28), channel_id=1, source_target_pairs={{0,1},{1,0},{2,3},{3,2},{4,5},{5,4},{6,7},{7,6},{8,9},{9,8},{10,11... | collective-permute-start | bytes 1474568 | tf_op jit(solution)/shard_map/ppermute | solution.py:51
  75.1 34.9 %collective-permute-start.7 = (bf16[6,64,640]{2,1,0:T(8,128)(2,1)S(1)}, bf16[6,64,640]{2,1,0:T(8,128)(2,1)S(1)}, u32[]{:S(2)}, u32[]{:S(2)}) collective-permute-start(bf16[6,64,640]{2,1,0:T(8,128)(2,1)S(1)} %get-tuple-element.29), channel_id=1, source_target_pairs={{1,2},{2,1},{3,4},{4,3},{5,6},{6,5},{7,8},{8,7},{9,10},{10,9},{11,... | collective-permute-start | bytes 1474568 | tf_op jit(solution)/shard_map/ppermute | solution.py:51
  80.3 30.6 %collective-permute-start.8 = (bf16[6,64,640]{2,1,0:T(8,128)(2,1)S(1)}, bf16[6,64,640]{2,1,0:T(8,128)(2,1)S(1)}, u32[]{:S(2)}, u32[]{:S(2)}) collective-permute-start(bf16[6,64,640]{2,1,0:T(8,128)(2,1)S(1)} %get-tuple-element.30), channel_id=1, source_target_pairs={{0,1},{1,0},{2,3},{3,2},{4,5},{5,4},{6,7},{7,6},{8,9},{9,8},{10,11... | collective-permute-start | bytes 1474568 | tf_op jit(solution)/shard_map/ppermute | solution.py:51
  97.6 15.7 %collective-permute-start.9 = (bf16[6,64,640]{2,1,0:T(8,128)(2,1)S(1)}, bf16[6,64,640]{2,1,0:T(8,128)(2,1)S(1)}, u32[]{:S(2)}, u32[]{:S(2)}) collective-permute-start(bf16[6,64,640]{2,1,0:T(8,128)(2,1)S(1)} %get-tuple-element.31), channel_id=1, source_target_pairs={{1,2},{2,1},{3,4},{4,3},{5,6},{6,5},{7,8},{8,7},{9,10},{10,9},{11,... | collective-permute-start | bytes 1474568 | tf_op jit(solution)/shard_map/ppermute | solution.py:51
  100.8 13.6 %collective-permute-start.12 = (bf16[6,64,640]{2,1,0:T(8,128)(2,1)S(1)}, bf16[6,64,640]{2,1,0:T(8,128)(2,1)S(1)}, u32[]{:S(2)}, u32[]{:S(2)}) collective-permute-start(bf16[6,64,640]{2,1,0:T(8,128)(2,1)S(1)} %get-tuple-element.34), channel_id=1, source_target_pairs={{0,1},{1,0},{2,3},{3,2},{4,5},{5,4},{6,7},{7,6},{8,9},{9,8},{10,11... | collective-permute-start | bytes 1474568 | tf_op jit(solution)/shard_map/ppermute | solution.py:51
  103.2 15.4 %collective-permute-start.13 = (bf16[6,64,640]{2,1,0:T(8,128)(2,1)S(1)}, bf16[6,64,640]{2,1,0:T(8,128)(2,1)S(1)}, u32[]{:S(2)}, u32[]{:S(2)}) collective-permute-start(bf16[6,64,640]{2,1,0:T(8,128)(2,1)S(1)} %get-tuple-element.35), channel_id=1, source_target_pairs={{1,2},{2,1},{3,4},{4,3},{5,6},{6,5},{7,8},{8,7},{9,10},{10,9},{11,... | collective-permute-start | bytes 1474568 | tf_op jit(solution)/shard_map/ppermute | solution.py:51
  113.3 5.3 %copy-start = (bf16[1,1,1,1024,1024]{4,3,2,1,0:T(8,128)(2,1)S(1)}, bf16[1,1,1,1024,1024]{4,3,2,1,0:T(8,128)(2,1)}, u32[]{:S(2)}) copy-start(bf16[1,1,1,1024,1024]{4,3,2,1,0:T(8,128)(2,1)} %param.3) | copy-start | bytes 6291460
where the time goes:
time: 123 us; the launch traced here: 122 us
  waiting for transfers between devices  55.9 us (45%)
  starting transfers between devices  50.4 us (41%)
  Pallas kernels  14.5 us (12%)
    ppermute x14, waiting for transfers between devices, swap(): got.append(lax.ppermute(value, axis, pairs))  55.9 us
    ppermute x14, starting transfers between devices, swap(): got.append(lax.ppermute(value, axis, pairs))  50.4 us
    pallas_call x10, Pallas kernels, call(): pl.pallas_call(kernel, out_shape=outs, in_specs=specs, out_specs=[far if...  14.5 us
  transfers between devices with their start and end apart: 14, of which 7 were waited for; matrix products, arithmetic and copies ran while one was open for 0% of the time, Pallas kernels for 5%

commit v1 on v0

--- a/solution.py
+++ b/solution.py
@@ -54,10 +54,15 @@
 
 def head_kernel(links, x, y, z, schur, vectors, top, bottom, near_a, far_a, matrix, right_side, sems):
     blocks = bottom.shape[0]
-    copies = [pltpu.make_async_copy(vectors, right_side, sems.at[blocks])]
-    for k in range(blocks):
-        rows = slice(k * BLOCK, (k + 1) * BLOCK)
-        copies.append(pltpu.make_async_copy(schur.at[rows, :], matrix.at[rows, :], sems.at[k]))
+    depth = vectors.shape[0] // 4
+    groups = [slice(i * depth, (i + 1) * depth) for i in range(4)]
+    copies = []
+    for i, rows in enumerate(groups):
+        copies.append(
+            pltpu.make_async_copy(vectors.at[rows, :], right_side.at[rows, :], sems.at[4 + i])
+        )
+    for i, rows in enumerate(groups):
+        copies.append(pltpu.make_async_copy(schur.at[rows, :], matrix.at[rows, :], sems.at[i]))
     for copy in copies:
         copy.start()
     lane = lax.broadcasted_iota(jnp.int32, (NOTE, top.shape[1]), 1)
@@ -65,19 +70,22 @@
     for i in range(LINKS):
         note = jnp.where(lane == i, links[i], note)
     top[blocks * HALF :, :] = note.astype(jnp.float32).astype(jnp.bfloat16)
-    copies[0].wait()
-    for k in range(blocks):
-        rows = slice(k * BLOCK, (k + 1) * BLOCK)
-        copies[k + 1].wait()
+    for copy in copies[:4]:
+        copy.wait()
+    for i, group in enumerate(groups):
+        copies[4 + i].wait()
         product = jnp.dot(
-            matrix[rows, :], right_side[...], preferred_element_type=jnp.float32
+            matrix[group, :], right_side[...], preferred_element_type=jnp.float32
         ).astype(jnp.bfloat16)
-        diagonal = matrix[rows, rows]
-        upper = slice(k * HALF, (k + 1) * HALF)
-        top[upper, BLOCK:] = product[:HALF]
-        top[upper, :BLOCK] = diagonal[:HALF]
-        bottom[k, :, BLOCK:] = product[HALF:]
-        bottom[k, :, :BLOCK] = diagonal[HALF:]
+        for j in range(depth // BLOCK):
+            k = i * (depth // BLOCK) + j
+            rows = slice(k * BLOCK, (k + 1) * BLOCK)
+            diagonal = matrix[rows, rows]
+            upper = slice(k * HALF, (k + 1) * HALF)
+            top[upper, BLOCK:] = product[j * BLOCK : j * BLOCK + HALF]
+            top[upper, :BLOCK] = diagonal[:HALF]
+            bottom[k, :, BLOCK:] = product[j * BLOCK + HALF : (j + 1) * BLOCK]
+            bottom[k, :, :BLOCK] = diagonal[HALF:]
     sx = side((x, y, z), 0)
     for a, out in ((sx, near_a), (-sx, far_a)):
         for b in STEPS:

time: 123 us -> 122 us (level)
  no operation moved by 1% of the time
where the time goes in v1:
time: 122 us
  waiting for transfers between devices  55.9 us (46%)
  starting transfers between devices  50.4 us (41%)
  Pallas kernels  13.9 us (11%)
    ppermute x14, waiting for transfers between devices, swap(): got.append(lax.ppermute(value, axis, pairs))  55.9 us
    ppermute x14, starting transfers between devices, swap(): got.append(lax.ppermute(value, axis, pairs))  50.4 us
    pallas_call x10, Pallas kernels, call(): pl.pallas_call(kernel, out_shape=outs, in_specs=specs, out_specs=[far if...  13.9 us
  transfers between devices with their start and end apart: 14, of which 7 were waited for; matrix products, arithmetic and copies ran while one was open for 0% of the time, Pallas kernels for 5%

profile of v1, /device:TPU:24, one launch (start us, length us, event | category | flops | bytes accessed | tf_op | source)
XLA Modules:
  0.0 121.7 jit_solution(12524437637675369323)
XLA Ops:
  0.6 0.0 copy-start.1
  0.6 0.6 copy-done.1
  1.3 3.9 %shard_map.50 = (bf16[528,640]{1,0:T(8,128)(2,1)S(1)}, bf16[8,64,640]{2,1,0:T(8,128)(2,1)S(1)}, bf16[9,64,640]{2,1,0:T(8,128)(2,1)S(1)}, bf16[9,64,640]{2,1,0:T(8,128)(2,1)S(1)}) custom-call(s32[26]{0:T(128)S(1)} %bitcast.10, s32[1]{0:T(128)} %bitcast.1.x, s32[1]{0:T(128)} %bitcast.2.y, s32[1]{0:T(128)} %bitcast.3.z, bf16[1024,1024]{1,0:T(8,128)(2,1)} %bitcast.8, ...), custom_call_target="tpu_custom_call" | custom-call | tf_op jit(solution)/shard_map/pallas_call | solution.py:279
  5.2 4.3 %collective-permute-start.4 = (bf16[9,64,640]{2,1,0:T(8,128)(2,1)S(1)}, bf16[9,64,640]{2,1,0:T(8,128)(2,1)S(1)}, u32[]{:S(2)}, u32[]{:S(2)}) collective-permute-start(bf16[9,64,640]{2,1,0:T(8,128)(2,1)S(1)} %get-tuple-element.26), channel_id=1, source_target_pairs={{0,64},{64,0},{128,192},{192,128},{256,320},{320,256},{384,448},{4... | collective-permute-start | bytes 2211848 | tf_op jit(solution)/shard_map/ppermute | solution.py:51
  9.5 9.1 %collective-permute-start.5 = (bf16[9,64,640]{2,1,0:T(8,128)(2,1)S(1)}, bf16[9,64,640]{2,1,0:T(8,128)(2,1)S(1)}, u32[]{:S(2)}, u32[]{:S(2)}) collective-permute-start(bf16[9,64,640]{2,1,0:T(8,128)(2,1)S(1)} %get-tuple-element.27), channel_id=1, source_target_pairs={{64,128},{128,64},{192,256},{256,192},{320,384},{384,320},{448,0},... | collective-permute-start | bytes 2211848 | tf_op jit(solution)/shard_map/ppermute | solution.py:51
  18.6 2.2 %collective-permute-start = (bf16[528,640]{1,0:T(8,128)(2,1)S(1)}, bf16[528,640]{1,0:T(8,128)(2,1)S(1)}, u32[]{:S(2)}, u32[]{:S(2)}) collective-permute-start(bf16[528,640]{1,0:T(8,128)(2,1)S(1)} %get-tuple-element.20.top), channel_id=1, source_target_pairs={{0,16},{16,0},{32,48},{48,32},{1,17},{17,1},{33,49},{49,33},{2,18}... | collective-permute-start | bytes 2027528 | tf_op jit(solution)/shard_map/ppermute | solution.py:51
  20.9 5.3 %collective-permute-start.1 = (bf16[528,640]{1,0:T(8,128)(2,1)S(1)}, bf16[528,640]{1,0:T(8,128)(2,1)S(1)}, u32[]{:S(2)}, u32[]{:S(2)}) collective-permute-start(bf16[528,640]{1,0:T(8,128)(2,1)S(1)} %get-tuple-element.20.top), channel_id=1, source_target_pairs={{16,32},{32,16},{17,33},{33,17},{18,34},{34,18},{19,35},{35,19},{2... | collective-permute-start | bytes 2027528 | tf_op jit(solution)/shard_map/ppermute | solution.py:51
  26.1 26.1 %collective-permute-done.near_b = bf16[528,640]{1,0:T(8,128)(2,1)S(1)} collective-permute-done((bf16[528,640]{1,0:T(8,128)(2,1)S(1)}, bf16[528,640]{1,0:T(8,128)(2,1)S(1)}, u32[]{:S(2)}, u32[]{:S(2)}) %collective-permute-start) | collective-permute-done | bytes 675872 | tf_op jit(solution)/shard_map/ppermute | solution.py:51
  52.2 3.0 %collective-permute-done.1.far_b = bf16[528,640]{1,0:T(8,128)(2,1)S(1)} collective-permute-done((bf16[528,640]{1,0:T(8,128)(2,1)S(1)}, bf16[528,640]{1,0:T(8,128)(2,1)S(1)}, u32[]{:S(2)}, u32[]{:S(2)}) %collective-permute-start.1) | collective-permute-done | bytes 675872 | tf_op jit(solution)/shard_map/ppermute | solution.py:51
  55.3 2.0 %shard_map.51 = (bf16[9,64,640]{2,1,0:T(8,128)(2,1)S(1)}, bf16[9,64,640]{2,1,0:T(8,128)(2,1)S(1)}, s32[8,128]{1,0:T(8,128)S(1)}, s32[8,128]{1,0:T(8,128)S(1)}) custom-call(s32[26]{0:T(128)S(1)} %bitcast.11, s32[1]{0:T(128)} %bitcast.1.x, s32[1]{0:T(128)} %bitcast.2.y, s32[1]{0:T(128)} %bitcast.3.z, bf16[528,640]{1,0:T(8,128)(2,1)S(1)} %get-tuple-element.20.top, ...), custom_call_target="tpu_custom_call" | custom-call | tf_op jit(solution)/shard_map/pallas_call | solution.py:279
  57.2 1.9 %collective-permute-start.2 = (bf16[9,64,640]{2,1,0:T(8,128)(2,1)S(1)}, bf16[9,64,640]{2,1,0:T(8,128)(2,1)S(1)}, u32[]{:S(2)}, u32[]{:S(2)}) collective-permute-start(bf16[9,64,640]{2,1,0:T(8,128)(2,1)S(1)} %get-tuple-element.23), channel_id=1, source_target_pairs={{0,64},{64,0},{128,192},{192,128},{256,320},{320,256},{384,448},{4... | collective-permute-start | bytes 2211848 | tf_op jit(solution)/shard_map/ppermute | solution.py:51
  59.2 3.7 %collective-permute-start.3 = (bf16[9,64,640]{2,1,0:T(8,128)(2,1)S(1)}, bf16[9,64,640]{2,1,0:T(8,128)(2,1)S(1)}, u32[]{:S(2)}, u32[]{:S(2)}) collective-permute-start(bf16[9,64,640]{2,1,0:T(8,128)(2,1)S(1)} %get-tuple-element.24), channel_id=1, source_target_pairs={{64,128},{128,64},{192,256},{256,192},{320,384},{384,320},{448,0},... | collective-permute-start | bytes 2211848 | tf_op jit(solution)/shard_map/ppermute | solution.py:51
  62.8 0.0 collective-permute-done.4.near_a
  62.9 0.0 collective-permute-done.5.far_a
  62.9 0.7 shard_map.56
  63.5 1.9 %collective-permute-start.10 = (bf16[9,64,640]{2,1,0:T(8,128)(2,1)S(1)}, bf16[9,64,640]{2,1,0:T(8,128)(2,1)S(1)}, u32[]{:S(2)}, u32[]{:S(2)}) collective-permute-start(bf16[9,64,640]{2,1,0:T(8,128)(2,1)S(1)} %get-tuple-element.32), channel_id=1, source_target_pairs={{0,16},{16,0},{32,48},{48,32},{1,17},{17,1},{33,49},{49,33},{2,18}... | collective-permute-start | bytes 2211848 | tf_op jit(solution)/shard_map/ppermute | solution.py:51
  65.5 2.6 %collective-permute-start.11 = (bf16[9,64,640]{2,1,0:T(8,128)(2,1)S(1)}, bf16[9,64,640]{2,1,0:T(8,128)(2,1)S(1)}, u32[]{:S(2)}, u32[]{:S(2)}) collective-permute-start(bf16[9,64,640]{2,1,0:T(8,128)(2,1)S(1)} %get-tuple-element.33), channel_id=1, source_target_pairs={{16,32},{32,16},{17,33},{33,17},{18,34},{34,18},{19,35},{35,19},{2... | collective-permute-start | bytes 2211848 | tf_op jit(solution)/shard_map/ppermute | solution.py:51
  68.1 0.8 shard_map.52
  68.8 1.9 %collective-permute-start.6 = (bf16[6,64,640]{2,1,0:T(8,128)(2,1)S(1)}, bf16[6,64,640]{2,1,0:T(8,128)(2,1)S(1)}, u32[]{:S(2)}, u32[]{:S(2)}) collective-permute-start(bf16[6,64,640]{2,1,0:T(8,128)(2,1)S(1)} %get-tuple-element.28), channel_id=1, source_target_pairs={{0,1},{1,0},{2,3},{3,2},{4,5},{5,4},{6,7},{7,6},{8,9},{9,8},{10,11... | collective-permute-start | bytes 1474568 | tf_op jit(solution)/shard_map/ppermute | solution.py:51
  70.7 3.7 %collective-permute-done.2.near.near_a = bf16[9,64,640]{2,1,0:T(8,128)(2,1)S(1)} collective-permute-done((bf16[9,64,640]{2,1,0:T(8,128)(2,1)S(1)}, bf16[9,64,640]{2,1,0:T(8,128)(2,1)S(1)}, u32[]{:S(2)}, u32[]{:S(2)}) %collective-permute-start.2) | collective-permute-done | bytes 737312 | tf_op jit(solution)/shard_map/ppermute | solution.py:51
  74.5 5.1 %collective-permute-start.7 = (bf16[6,64,640]{2,1,0:T(8,128)(2,1)S(1)}, bf16[6,64,640]{2,1,0:T(8,128)(2,1)S(1)}, u32[]{:S(2)}, u32[]{:S(2)}) collective-permute-start(bf16[6,64,640]{2,1,0:T(8,128)(2,1)S(1)} %get-tuple-element.29), channel_id=1, source_target_pairs={{1,2},{2,1},{3,4},{4,3},{5,6},{6,5},{7,8},{8,7},{9,10},{10,9},{11,... | collective-permute-start | bytes 1474568 | tf_op jit(solution)/shard_map/ppermute | solution.py:51
  79.5 0.0 collective-permute-done.3.far.far_a
  79.6 0.1 shard_map.53
  79.7 1.9 %collective-permute-start.8 = (bf16[6,64,640]{2,1,0:T(8,128)(2,1)S(1)}, bf16[6,64,640]{2,1,0:T(8,128)(2,1)S(1)}, u32[]{:S(2)}, u32[]{:S(2)}) collective-permute-start(bf16[6,64,640]{2,1,0:T(8,128)(2,1)S(1)} %get-tuple-element.30), channel_id=1, source_target_pairs={{0,1},{1,0},{2,3},{3,2},{4,5},{5,4},{6,7},{7,6},{8,9},{9,8},{10,11... | collective-permute-start | bytes 1474568 | tf_op jit(solution)/shard_map/ppermute | solution.py:51
  81.6 15.4 %collective-permute-done.10.near_b.near = bf16[9,64,640]{2,1,0:T(8,128)(2,1)S(1)} collective-permute-done((bf16[9,64,640]{2,1,0:T(8,128)(2,1)S(1)}, bf16[9,64,640]{2,1,0:T(8,128)(2,1)S(1)}, u32[]{:S(2)}, u32[]{:S(2)}) %collective-permute-start.10) | collective-permute-done | bytes 737312 | tf_op jit(solution)/shard_map/ppermute | solution.py:51
  97.0 2.0 %collective-permute-start.9 = (bf16[6,64,640]{2,1,0:T(8,128)(2,1)S(1)}, bf16[6,64,640]{2,1,0:T(8,128)(2,1)S(1)}, u32[]{:S(2)}, u32[]{:S(2)}) collective-permute-start(bf16[6,64,640]{2,1,0:T(8,128)(2,1)S(1)} %get-tuple-element.31), channel_id=1, source_target_pairs={{1,2},{2,1},{3,4},{4,3},{5,6},{6,5},{7,8},{8,7},{9,10},{10,9},{11,... | collective-permute-start | bytes 1474568 | tf_op jit(solution)/shard_map/ppermute | solution.py:51
  99.0 1.1 collective-permute-done.11.far_b.far
  100.1 0.1 shard_map.58
  100.2 2.3 %collective-permute-start.12 = (bf16[6,64,640]{2,1,0:T(8,128)(2,1)S(1)}, bf16[6,64,640]{2,1,0:T(8,128)(2,1)S(1)}, u32[]{:S(2)}, u32[]{:S(2)}) collective-permute-start(bf16[6,64,640]{2,1,0:T(8,128)(2,1)S(1)} %get-tuple-element.34), channel_id=1, source_target_pairs={{0,1},{1,0},{2,3},{3,2},{4,5},{5,4},{6,7},{7,6},{8,9},{9,8},{10,11... | collective-permute-start | bytes 1474568 | tf_op jit(solution)/shard_map/ppermute | solution.py:51
  102.5 0.0 collective-permute-done.6.near_ahead
  102.6 6.2 %collective-permute-start.13 = (bf16[6,64,640]{2,1,0:T(8,128)(2,1)S(1)}, bf16[6,64,640]{2,1,0:T(8,128)(2,1)S(1)}, u32[]{:S(2)}, u32[]{:S(2)}) collective-permute-start(bf16[6,64,640]{2,1,0:T(8,128)(2,1)S(1)} %get-tuple-element.35), channel_id=1, source_target_pairs={{1,2},{2,1},{3,4},{4,3},{5,6},{6,5},{7,8},{8,7},{9,10},{10,9},{11,... | collective-permute-start | bytes 1474568 | tf_op jit(solution)/shard_map/ppermute | solution.py:51
  108.8 0.7 shard_map.55.seed
  109.4 0.0 collective-permute-done.7.far_ahead
  109.4 0.8 shard_map.57.lower
  110.3 0.0 collective-permute-done.8.near_c
  110.3 2.4 %collective-permute-done.9.far_c = bf16[6,64,640]{2,1,0:T(8,128)(2,1)S(1)} collective-permute-done((bf16[6,64,640]{2,1,0:T(8,128)(2,1)S(1)}, bf16[6,64,640]{2,1,0:T(8,128)(2,1)S(1)}, u32[]{:S(2)}, u32[]{:S(2)}) %collective-permute-start.9) | collective-permute-done | bytes 491552 | tf_op jit(solution)/shard_map/ppermute | solution.py:51
  112.7 0.0 copy-start
  112.7 1.2 shard_map.54.upper
  113.8 0.0 collective-permute-done.12.near_c
  113.8 4.1 %collective-permute-done.13.far_c = bf16[6,64,640]{2,1,0:T(8,128)(2,1)S(1)} collective-permute-done((bf16[6,64,640]{2,1,0:T(8,128)(2,1)S(1)}, bf16[6,64,640]{2,1,0:T(8,128)(2,1)S(1)}, u32[]{:S(2)}, u32[]{:S(2)}) %collective-permute-start.13) | collective-permute-done | bytes 491552 | tf_op jit(solution)/shard_map/ppermute | solution.py:51
  117.9 0.0 copy-done
  117.9 3.8 %shard_map.59 = (bf16[1024,512]{1,0:T(8,128)(2,1)}, bf16[1024,512]{1,0:T(8,128)(2,1)}) custom-call(s32[26]{0:T(128)S(1)} %bitcast.17, s32[1]{0:T(128)} %bitcast.1.x, s32[1]{0:T(128)} %bitcast.2.y, s32[1]{0:T(128)} %bitcast.3.z, f32[8,64,640]{2,1,0:T(8,128)S(1)} %shard_map.54.upper, f32[8,64,640]{2,1,0:T(8,128)S(1)} %shard_map.57.lower, ...), custom_call_target="tpu_custom_call" | custom-call | tf_op jit(solution)/shard_map/pallas_call | solution.py:279
Async XLA Ops:
  0.6 0.7 copy-start.1
  5.2 57.6 %collective-permute-start.4 = (bf16[9,64,640]{2,1,0:T(8,128)(2,1)S(1)}, bf16[9,64,640]{2,1,0:T(8,128)(2,1)S(1)}, u32[]{:S(2)}, u32[]{:S(2)}) collective-permute-start(bf16[9,64,640]{2,1,0:T(8,128)(2,1)S(1)} %get-tuple-element.26), channel_id=1, source_target_pairs={{0,64},{64,0},{128,192},{192,128},{256,320},{320,256},{384,448},{4... | collective-permute-start | bytes 2211848 | tf_op jit(solution)/shard_map/ppermute | solution.py:51
  9.5 53.4 %collective-permute-start.5 = (bf16[9,64,640]{2,1,0:T(8,128)(2,1)S(1)}, bf16[9,64,640]{2,1,0:T(8,128)(2,1)S(1)}, u32[]{:S(2)}, u32[]{:S(2)}) collective-permute-start(bf16[9,64,640]{2,1,0:T(8,128)(2,1)S(1)} %get-tuple-element.27), channel_id=1, source_target_pairs={{64,128},{128,64},{192,256},{256,192},{320,384},{384,320},{448,0},... | collective-permute-start | bytes 2211848 | tf_op jit(solution)/shard_map/ppermute | solution.py:51
  18.6 33.6 %collective-permute-start = (bf16[528,640]{1,0:T(8,128)(2,1)S(1)}, bf16[528,640]{1,0:T(8,128)(2,1)S(1)}, u32[]{:S(2)}, u32[]{:S(2)}) collective-permute-start(bf16[528,640]{1,0:T(8,128)(2,1)S(1)} %get-tuple-element.20.top), channel_id=1, source_target_pairs={{0,16},{16,0},{32,48},{48,32},{1,17},{17,1},{33,49},{49,33},{2,18}... | collective-permute-start | bytes 2027528 | tf_op jit(solution)/shard_map/ppermute | solution.py:51
  20.9 34.4 %collective-permute-start.1 = (bf16[528,640]{1,0:T(8,128)(2,1)S(1)}, bf16[528,640]{1,0:T(8,128)(2,1)S(1)}, u32[]{:S(2)}, u32[]{:S(2)}) collective-permute-start(bf16[528,640]{1,0:T(8,128)(2,1)S(1)} %get-tuple-element.20.top), channel_id=1, source_target_pairs={{16,32},{32,16},{17,33},{33,17},{18,34},{34,18},{19,35},{35,19},{2... | collective-permute-start | bytes 2027528 | tf_op jit(solution)/shard_map/ppermute | solution.py:51
  57.2 17.2 %collective-permute-start.2 = (bf16[9,64,640]{2,1,0:T(8,128)(2,1)S(1)}, bf16[9,64,640]{2,1,0:T(8,128)(2,1)S(1)}, u32[]{:S(2)}, u32[]{:S(2)}) collective-permute-start(bf16[9,64,640]{2,1,0:T(8,128)(2,1)S(1)} %get-tuple-element.23), channel_id=1, source_target_pairs={{0,64},{64,0},{128,192},{192,128},{256,320},{320,256},{384,448},{4... | collective-permute-start | bytes 2211848 | tf_op jit(solution)/shard_map/ppermute | solution.py:51
  59.2 20.4 %collective-permute-start.3 = (bf16[9,64,640]{2,1,0:T(8,128)(2,1)S(1)}, bf16[9,64,640]{2,1,0:T(8,128)(2,1)S(1)}, u32[]{:S(2)}, u32[]{:S(2)}) collective-permute-start(bf16[9,64,640]{2,1,0:T(8,128)(2,1)S(1)} %get-tuple-element.24), channel_id=1, source_target_pairs={{64,128},{128,64},{192,256},{256,192},{320,384},{384,320},{448,0},... | collective-permute-start | bytes 2211848 | tf_op jit(solution)/shard_map/ppermute | solution.py:51
  63.5 33.5 %collective-permute-start.10 = (bf16[9,64,640]{2,1,0:T(8,128)(2,1)S(1)}, bf16[9,64,640]{2,1,0:T(8,128)(2,1)S(1)}, u32[]{:S(2)}, u32[]{:S(2)}) collective-permute-start(bf16[9,64,640]{2,1,0:T(8,128)(2,1)S(1)} %get-tuple-element.32), channel_id=1, source_target_pairs={{0,16},{16,0},{32,48},{48,32},{1,17},{17,1},{33,49},{49,33},{2,18}... | collective-permute-start | bytes 2211848 | tf_op jit(solution)/shard_map/ppermute | solution.py:51
  65.5 34.6 %collective-permute-start.11 = (bf16[9,64,640]{2,1,0:T(8,128)(2,1)S(1)}, bf16[9,64,640]{2,1,0:T(8,128)(2,1)S(1)}, u32[]{:S(2)}, u32[]{:S(2)}) collective-permute-start(bf16[9,64,640]{2,1,0:T(8,128)(2,1)S(1)} %get-tuple-element.33), channel_id=1, source_target_pairs={{16,32},{32,16},{17,33},{33,17},{18,34},{34,18},{19,35},{35,19},{2... | collective-permute-start | bytes 2211848 | tf_op jit(solution)/shard_map/ppermute | solution.py:51
  68.8 33.7 %collective-permute-start.6 = (bf16[6,64,640]{2,1,0:T(8,128)(2,1)S(1)}, bf16[6,64,640]{2,1,0:T(8,128)(2,1)S(1)}, u32[]{:S(2)}, u32[]{:S(2)}) collective-permute-start(bf16[6,64,640]{2,1,0:T(8,128)(2,1)S(1)} %get-tuple-element.28), channel_id=1, source_target_pairs={{0,1},{1,0},{2,3},{3,2},{4,5},{5,4},{6,7},{7,6},{8,9},{9,8},{10,11... | collective-permute-start | bytes 1474568 | tf_op jit(solution)/shard_map/ppermute | solution.py:51
  74.5 35.0 %collective-permute-start.7 = (bf16[6,64,640]{2,1,0:T(8,128)(2,1)S(1)}, bf16[6,64,640]{2,1,0:T(8,128)(2,1)S(1)}, u32[]{:S(2)}, u32[]{:S(2)}) collective-permute-start(bf16[6,64,640]{2,1,0:T(8,128)(2,1)S(1)} %get-tuple-element.29), channel_id=1, source_target_pairs={{1,2},{2,1},{3,4},{4,3},{5,6},{6,5},{7,8},{8,7},{9,10},{10,9},{11,... | collective-permute-start | bytes 1474568 | tf_op jit(solution)/shard_map/ppermute | solution.py:51
  79.7 30.6 %collective-permute-start.8 = (bf16[6,64,640]{2,1,0:T(8,128)(2,1)S(1)}, bf16[6,64,640]{2,1,0:T(8,128)(2,1)S(1)}, u32[]{:S(2)}, u32[]{:S(2)}) collective-permute-start(bf16[6,64,640]{2,1,0:T(8,128)(2,1)S(1)} %get-tuple-element.30), channel_id=1, source_target_pairs={{0,1},{1,0},{2,3},{3,2},{4,5},{5,4},{6,7},{7,6},{8,9},{9,8},{10,11... | collective-permute-start | bytes 1474568 | tf_op jit(solution)/shard_map/ppermute | solution.py:51
  97.0 15.7 %collective-permute-start.9 = (bf16[6,64,640]{2,1,0:T(8,128)(2,1)S(1)}, bf16[6,64,640]{2,1,0:T(8,128)(2,1)S(1)}, u32[]{:S(2)}, u32[]{:S(2)}) collective-permute-start(bf16[6,64,640]{2,1,0:T(8,128)(2,1)S(1)} %get-tuple-element.31), channel_id=1, source_target_pairs={{1,2},{2,1},{3,4},{4,3},{5,6},{6,5},{7,8},{8,7},{9,10},{10,9},{11,... | collective-permute-start | bytes 1474568 | tf_op jit(solution)/shard_map/ppermute | solution.py:51
  100.2 13.6 %collective-permute-start.12 = (bf16[6,64,640]{2,1,0:T(8,128)(2,1)S(1)}, bf16[6,64,640]{2,1,0:T(8,128)(2,1)S(1)}, u32[]{:S(2)}, u32[]{:S(2)}) collective-permute-start(bf16[6,64,640]{2,1,0:T(8,128)(2,1)S(1)} %get-tuple-element.34), channel_id=1, source_target_pairs={{0,1},{1,0},{2,3},{3,2},{4,5},{5,4},{6,7},{7,6},{8,9},{9,8},{10,11... | collective-permute-start | bytes 1474568 | tf_op jit(solution)/shard_map/ppermute | solution.py:51
  102.6 15.4 %collective-permute-start.13 = (bf16[6,64,640]{2,1,0:T(8,128)(2,1)S(1)}, bf16[6,64,640]{2,1,0:T(8,128)(2,1)S(1)}, u32[]{:S(2)}, u32[]{:S(2)}) collective-permute-start(bf16[6,64,640]{2,1,0:T(8,128)(2,1)S(1)} %get-tuple-element.35), channel_id=1, source_target_pairs={{1,2},{2,1},{3,4},{4,3},{5,6},{6,5},{7,8},{8,7},{9,10},{10,9},{11,... | collective-permute-start | bytes 1474568 | tf_op jit(solution)/shard_map/ppermute | solution.py:51
  112.7 5.3 %copy-start = (bf16[1,1,1,1024,1024]{4,3,2,1,0:T(8,128)(2,1)S(1)}, bf16[1,1,1,1024,1024]{4,3,2,1,0:T(8,128)(2,1)}, u32[]{:S(2)}) copy-start(bf16[1,1,1,1024,1024]{4,3,2,1,0:T(8,128)(2,1)} %param.3) | copy-start | bytes 6291460
